TPU v7x, 128 devices: a whole 4x4x4 slice. The times are simulated.
128 devices in a mesh: front: 4 (over x_lo, core), row: 4 (over z), col: 8 (over y, x_hi).
Axes of the slice: x: 4 (x_hi: 2, x_lo: 2; x = x_hi * 2 + x_lo), y: 4, z: 4, core: 2. Of those that a mesh axis runs over, the one named last changes fastest.
Arguments:
- front_entries: float32 [4, 8192, 8192], P('front', 'row', 'col'), may hold values from -12 to 128, as said below
- kid_u: bfloat16 [16, 4096, 128], P('front', ('row', 'col')), may hold values from -0.7109375 to 0.7109375
- kid_v: bfloat16 [16, 4096, 128], P('front', ('row', 'col')), may hold values from -0.7109375 to 0.7109375
- kid_d: bfloat16 [16, 4096, 256], P('front', ('row', 'col')), may hold values from -2.09375 to 2.09375
- kid_counts: int32 [16], replicated, may hold values from 32 to 128
- kid_blocks: int32 [16, 16], replicated, may hold values from 0 to 31, as said below
Outputs:
- front_out: float32 [4, 8192, 8192], P('front', 'row', 'col')
Inputs may be any that keep to these rules, and one draw needn't show every extreme that they name: `front_entries`: diagonal entries lie between 64 and 128; the other entries are of order one. `kid_blocks`: each row holds distinct block positions in increasing order. `kid_counts`: rank columns at or beyond a child's count are padding.
All inputs are finite; a program needn't handle non-finite values.
Results may differ from a plain program's by a relative error of at most 0.004.
Values may be sent and summed in bfloat16 or wider, within the bound.
No kernel may reach another device: no remote copies, remote signals or barrier semaphores. Data moves between devices by JAX's collectives and lax.ppermute only.
A program may use at most 128 MiB of HBM per device.

v0:
```python
import jax
import jax.numpy as jnp
from jax import lax
from jax.sharding import Mesh
from jax.sharding import PartitionSpec as P

PANEL = 256
PANELS = 4
COL = ("col_0", "col_1")
ROW_COL = ("row", "col_0", "col_1")


def shifted(value, axis, by):
    peers = lax.axis_size(axis)
    return lax.ppermute(value, axis, [(i, (i + by) % peers) for i in range(peers)])


def from_root(value, axis, root):
    return lax.dynamic_index_in_dim(lax.all_gather(value, axis), root, 0, keepdims=False)


def broadcast_by_axis(value, axes, root):
    value = jnp.where(lax.axis_index(axes) == root, value, jnp.zeros_like(value))
    for axis in axes:
        value = lax.psum(value, axis)
    return value


def invert(block):
    gram = jnp.dot(block.T, block, precision=lax.Precision.HIGHEST)
    factor = jnp.linalg.cholesky(gram)
    return jax.scipy.linalg.cho_solve((factor, True), block.T)


def make_collector(blocks, row_offset, col_offset, row_width, col_width, rank_width, leaf_width):
    children = blocks.shape[0]
    block_count = blocks.shape[1]

    def place_rows(carry, piece, start):
        rows_u, cols_v, rows_d = carry
        length = piece.shape[1]
        child_rows = jnp.arange(length, dtype=jnp.int32)
        which_block = child_rows // leaf_width
        within = child_rows % leaf_width
        onehot = (which_block[:, None] == jnp.arange(block_count, dtype=jnp.int32)[None, :]).astype(
            jnp.int32
        )
        target = (
            jnp.sum(blocks[:, None, :] * onehot[None, :, :], axis=2) * leaf_width + within[None, :]
        )
        local_row = target - row_offset
        local_row = jnp.where((local_row >= 0) & (local_row < row_width), local_row, row_width)
        local_col = target - col_offset
        local_col = jnp.where((local_col >= 0) & (local_col < col_width), local_col, col_width)
        child_index = jnp.broadcast_to(jnp.arange(children, dtype=jnp.int32)[:, None], target.shape)
        rows_u = rows_u.at[local_row, child_index].set(piece[:, :, :rank_width], mode="drop")
        cols_v = cols_v.at[local_col, child_index].set(
            piece[:, :, rank_width : 2 * rank_width], mode="drop"
        )
        rows_d = rows_d.at[local_row].add(
            piece[:, :, 2 * rank_width :].astype(jnp.float32), mode="drop"
        )
        return (rows_u, cols_v, rows_d)

    empty_carry = (
        jnp.zeros((row_width, children, rank_width), jnp.bfloat16),
        jnp.zeros((col_width, children, rank_width), jnp.bfloat16),
        jnp.zeros((row_width, leaf_width), jnp.float32),
    )
    return (place_rows, empty_carry)


def expand_tile(collected, counts, row_offset, col_offset, leaf_width):
    rows_u, cols_v, rows_d = collected
    row_width, children, rank_width = rows_u.shape
    col_width = cols_v.shape[0]
    rank_mask = (jnp.arange(rank_width, dtype=jnp.int32)[None, :] < counts[:, None]).astype(
        jnp.bfloat16
    )
    masked_u = (rows_u * rank_mask[None, :, :]).reshape(row_width, children * rank_width)
    lowrank = lax.dot_general(
        masked_u,
        cols_v.reshape(col_width, children * rank_width),
        (((1,), (1,)), ((), ())),
        preferred_element_type=jnp.float32,
    )
    row_leaves = row_width // leaf_width
    col_leaves = col_width // leaf_width
    row_blocks = row_offset // leaf_width + jnp.arange(row_leaves, dtype=jnp.int32)
    col_blocks = col_offset // leaf_width + jnp.arange(col_leaves, dtype=jnp.int32)
    same_block = (row_blocks[:, None] == col_blocks[None, :]).astype(jnp.float32)
    stacked_d = rows_d.reshape(row_leaves, leaf_width, leaf_width)
    diagonal_part = (stacked_d[:, :, None, :] * same_block[:, None, :, None]).reshape(
        row_width, col_width
    )
    return lowrank + diagonal_part


def local(front_entries, kid_u, kid_v, kid_d, kid_counts, kid_blocks):
    children = kid_u.shape[0]
    rank_width = kid_u.shape[2]
    leaf_width = kid_d.shape[2]
    row_width = front_entries.shape[1]
    col_width = front_entries.shape[2]
    row_offset = lax.axis_index("row") * row_width
    col_offset = lax.axis_index(COL) * col_width
    front_count = lax.axis_size("front")
    packed = jnp.concatenate((kid_u, kid_v, kid_d), axis=2)
    moved = shifted(packed, "front", 1)
    first_child = (lax.axis_index("front") + front_count - 1) % front_count * children
    counts = lax.dynamic_slice_in_dim(kid_counts, first_child, children, 0)
    blocks = lax.dynamic_slice_in_dim(kid_blocks, first_child, children, 0)
    place_rows, empty_carry = make_collector(
        blocks, row_offset, col_offset, row_width, col_width, rank_width, leaf_width
    )
    collected = place_rows(
        empty_carry, lax.all_gather(moved, ROW_COL, axis=1, tiled=True), jnp.int32(0)
    )
    front = front_entries[0] + expand_tile(collected, counts, row_offset, col_offset, leaf_width)
    row_ids = row_offset + jnp.arange(row_width, dtype=jnp.int32)
    col_ids = col_offset + jnp.arange(col_width, dtype=jnp.int32)
    first_column = lax.axis_index(COL) == 0
    identity = jnp.eye(PANEL, dtype=jnp.float32)
    for panel_index in range(PANELS):
        start = panel_index * PANEL
        finish = start + PANEL
        rows_now = from_root(front[start:finish, :].astype(jnp.bfloat16), "row", 0).astype(
            jnp.float32
        )
        pivot = jnp.where(first_column, rows_now[:, start:finish], identity)
        inverse = invert(pivot)
        below = (row_ids >= finish)[:, None]
        lower = jnp.where(
            below, jnp.dot(front[:, start:finish], inverse, precision=lax.Precision.HIGHEST), 0.0
        )
        lower_b = broadcast_by_axis(lower.astype(jnp.bfloat16), COL, 0)
        upper_b = jnp.where((col_ids >= finish)[None, :], rows_now, 0.0).astype(jnp.bfloat16)
        front = front - jnp.dot(lower_b, upper_b, preferred_element_type=jnp.float32)
        front = front.at[:, start:finish].set(
            jnp.where(below & first_column, lower, front[:, start:finish])
        )
    return front[None]


def solution(mesh):
    finer = Mesh(
        mesh.devices.reshape(mesh.shape["front"], mesh.shape["row"], 4, 2),
        ("front", "row", "col_0", "col_1"),
    )
    in_specs = (
        P("front", "row", COL),
        P("front", ROW_COL, None),
        P("front", ROW_COL, None),
        P("front", ROW_COL, None),
        P(),
        P(),
    )
    out_specs = P("front", "row", COL)
    return jax.shard_map(local, mesh=finer, in_specs=in_specs, out_specs=out_specs, check_vma=False)
```

profile of v0, /device:TPU:1, one launch (start us, length us, event | category | flops | bytes accessed | tf_op | source)
XLA Modules:
  0.0 1218.4 jit_solution(10147357242169241187)
XLA Ops:
  18.6 157.3 %all-gather.10.cloned.1.call-done = bf16[4,4096,512]{2,1,0:T(8,128)(2,1)} async-done(((bf16[4,128,512]{2,1,0:T(8,128)(2,1)}), bf16[4,4096,512]{2,1,0:T(8,128)(2,1)}) %all-gather.10.cloned.1.call-update) | async-done | bytes 16777232 | tf_op jit(solution)/shard_map/all_gather | solution.py:117
  183.2 81.0 %scatter_custom_fusion = f32[2048,256]{1,0:T(8,128)S(1)} fusion(s32[16384]{0:T(1024)S(1)} %bitcast.206, bf16[16384,256]{1,0:T(8,128)(2,1)} %bitcast.198, f32[]{:T(128)} %constant.285.clone.1), kind=kCustom, calls=%fused_computation.11 | custom fusion | flops 8388608 | bytes 10485764 | tf_op jit(solution)/shard_map/scatter-add | solution.py:60
  283.6 43.2 %scatter_custom_fusion.1 = bf16[8192,128]{1,0:T(8,128)(2,1)} fusion(s32[16384]{0:T(1024)S(1)} %bitcast.208, bf16[16384,128]{1,0:T(8,128)(2,1)} %bitcast.204, bf16[]{:T(256)} %constant.269.clone.1), kind=kCustom, calls=%fused_computation.55 | custom fusion | bytes 2097664
  328.5 41.6 %scatter_custom_fusion.2 = bf16[4096,128]{1,0:T(8,128)(2,1)S(1)} fusion(s32[16384]{0:T(1024)S(1)} %bitcast.207, bf16[16384,128]{1,0:T(8,128)(2,1)} %bitcast.203, bf16[]{:T(256)} %constant.269.clone.1), kind=kCustom, calls=%fused_computation.77 | custom fusion | bytes 1049088
  383.1 29.5 %all-gather.12.cloned.1.call-done = bf16[1024,1024]{1,0:T(8,128)(2,1)} async-done(((bf16[256,1024]{1,0:T(8,128)(2,1)}), bf16[1024,1024]{1,0:T(8,128)(2,1)}) %all-gather.12.cloned.1.call-update) | async-done | bytes 2097168 | tf_op jit(solution)/shard_map/all_gather | solution.py:19
  436.6 11.7 cholesky.231
  455.4 19.7 %custom-call.20 = f32[2,128,128]{1,2,0:T(8,128)S(1)} custom-call(f32[2,128,128]{2,1,0:T(8,128)S(1)} %get-tuple-element.81), custom_call_target="InvertDiagBlocksLowerTriangular" | custom-call | tf_op jit(solution)/shard_map/jit(_cho_solve)/triangular_solve | solution.py:32
  481.5 44.4 %all-reduce.10.cloned.1.call-done = bf16[2048,256]{1,0:T(8,128)(2,1)} async-done(((bf16[2048,256]{1,0:T(8,128)(2,1)}), bf16[2048,256]{1,0:T(8,128)(2,1)}) %all-reduce.10.cloned.1.call-update) | async-done | bytes 1048592 | tf_op jit(solution)/shard_map/psum | solution.py:25
  526.6 52.4 %all-reduce.12.cloned.1.call-done = bf16[2048,256]{1,0:T(8,128)(2,1)} async-done(((bf16[2048,256]{1,0:T(8,128)(2,1)}), bf16[2048,256]{1,0:T(8,128)(2,1)}) %all-reduce.12.cloned.1.call-update) | async-done | bytes 1048592 | tf_op jit(solution)/shard_map/psum | solution.py:25
  589.9 30.4 %all-gather.14.cloned.1.call-done = bf16[1024,1024]{1,0:T(8,128)(2,1)} async-done(((bf16[256,1024]{1,0:T(8,128)(2,1)}), bf16[1024,1024]{1,0:T(8,128)(2,1)}) %all-gather.14.cloned.1.call-update) | async-done | bytes 2097168 | tf_op jit(solution)/shard_map/all_gather | solution.py:19
  644.3 11.7 cholesky.265
  662.7 19.7 %custom-call.22 = f32[2,128,128]{1,2,0:T(8,128)S(1)} custom-call(f32[2,128,128]{2,1,0:T(8,128)S(1)} %get-tuple-element.82), custom_call_target="InvertDiagBlocksLowerTriangular" | custom-call | tf_op jit(solution)/shard_map/jit(_cho_solve)/triangular_solve | solution.py:32
  688.8 44.3 %all-reduce.14.cloned.1.call-done = bf16[2048,256]{1,0:T(8,128)(2,1)} async-done(((bf16[2048,256]{1,0:T(8,128)(2,1)}), bf16[2048,256]{1,0:T(8,128)(2,1)}) %all-reduce.14.cloned.1.call-update) | async-done | bytes 1048592 | tf_op jit(solution)/shard_map/psum | solution.py:25
  733.9 52.5 %all-reduce.16.cloned.1.call-done = bf16[2048,256]{1,0:T(8,128)(2,1)} async-done(((bf16[2048,256]{1,0:T(8,128)(2,1)}), bf16[2048,256]{1,0:T(8,128)(2,1)}) %all-reduce.16.cloned.1.call-update) | async-done | bytes 1048592 | tf_op jit(solution)/shard_map/psum | solution.py:25
  797.5 30.1 %all-gather.16.cloned.1.call-done = bf16[1024,1024]{1,0:T(8,128)(2,1)} async-done(((bf16[256,1024]{1,0:T(8,128)(2,1)}), bf16[1024,1024]{1,0:T(8,128)(2,1)}) %all-gather.16.cloned.1.call-update) | async-done | bytes 2097168 | tf_op jit(solution)/shard_map/all_gather | solution.py:19
  851.7 11.7 cholesky.299
  870.1 19.7 %custom-call.24 = f32[2,128,128]{1,2,0:T(8,128)S(1)} custom-call(f32[2,128,128]{2,1,0:T(8,128)S(1)} %get-tuple-element.83), custom_call_target="InvertDiagBlocksLowerTriangular" | custom-call | tf_op jit(solution)/shard_map/jit(_cho_solve)/triangular_solve | solution.py:32
  896.3 44.4 %all-reduce.18.cloned.1.call-done = bf16[2048,256]{1,0:T(8,128)(2,1)} async-done(((bf16[2048,256]{1,0:T(8,128)(2,1)}), bf16[2048,256]{1,0:T(8,128)(2,1)}) %all-reduce.18.cloned.1.call-update) | async-done | bytes 1048592 | tf_op jit(solution)/shard_map/psum | solution.py:25
  941.4 52.3 %all-reduce.20.cloned.1.call-done = bf16[2048,256]{1,0:T(8,128)(2,1)} async-done(((bf16[2048,256]{1,0:T(8,128)(2,1)}), bf16[2048,256]{1,0:T(8,128)(2,1)}) %all-reduce.20.cloned.1.call-update) | async-done | bytes 1048592 | tf_op jit(solution)/shard_map/psum | solution.py:25
  1004.7 30.3 %all-gather.18.cloned.1.call-done = bf16[1024,1024]{1,0:T(8,128)(2,1)} async-done(((bf16[256,1024]{1,0:T(8,128)(2,1)}), bf16[1024,1024]{1,0:T(8,128)(2,1)}) %all-gather.18.cloned.1.call-update) | async-done | bytes 2097168 | tf_op jit(solution)/shard_map/all_gather | solution.py:19
  1059.1 11.7 cholesky.333
  1077.6 19.7 %custom-call.26 = f32[2,128,128]{1,2,0:T(8,128)S(1)} custom-call(f32[2,128,128]{2,1,0:T(8,128)S(1)} %get-tuple-element.84), custom_call_target="InvertDiagBlocksLowerTriangular" | custom-call | tf_op jit(solution)/shard_map/jit(_cho_solve)/triangular_solve | solution.py:32
  1103.7 44.4 %all-reduce.22.cloned.1.call-done = bf16[2048,256]{1,0:T(8,128)(2,1)} async-done(((bf16[2048,256]{1,0:T(8,128)(2,1)}), bf16[2048,256]{1,0:T(8,128)(2,1)}) %all-reduce.22.cloned.1.call-update) | async-done | bytes 1048592 | tf_op jit(solution)/shard_map/psum | solution.py:25
  1148.1 53.2 %all-reduce.24.cloned.1.call-done = bf16[2048,256]{1,0:T(8,128)(2,1)} async-done(((bf16[2048,256]{1,0:T(8,128)(2,1)}), bf16[2048,256]{1,0:T(8,128)(2,1)}) %all-reduce.24.cloned.1.call-update) | async-done | bytes 1048592 | tf_op jit(solution)/shard_map/psum | solution.py:25
  (230 shorter events, 257.3 us)
Async XLA Ops:
  6.5 10.9 copy-start
  6.5 11.3 copy-start.9
  6.5 11.5 copy-start.7
  6.5 11.5 copy-start.8
  6.5 11.8 copy-start.10
  6.5 169.3 %all-gather.10.cloned.1.call-start = ((), (), s32[]{:S(2)}) async-start(), calls=%async_computation | async-start | bytes 17301504 | tf_op jit(solution)/shard_map/all_gather | solution.py:117
  7.7 8.8 collective-permute-start
  17.3 395.3 %all-gather.12.cloned.1.call-start = ((), (), s32[]{:S(2)}) async-start(), calls=%async_computation.9 | async-start | bytes 2621440 | tf_op jit(solution)/shard_map/all_gather | solution.py:19
  378.7 3.4 copy-start.5
  383.0 142.9 %all-reduce.10.cloned.1.call-start = ((), (), s32[]{:S(2)}) async-start(), calls=%async_computation.1 | async-start | bytes 2097152 | tf_op jit(solution)/shard_map/psum | solution.py:25
  481.4 97.5 %all-reduce.12.cloned.1.call-start = ((), (), s32[]{:S(2)}) async-start(), calls=%async_computation.2 | async-start | bytes 2097152 | tf_op jit(solution)/shard_map/psum | solution.py:25
  525.8 94.4 %all-gather.14.cloned.1.call-start = ((), (), s32[]{:S(2)}) async-start(), calls=%async_computation.10 | async-start | bytes 2621440 | tf_op jit(solution)/shard_map/all_gather | solution.py:19
  585.3 3.4 copy-start.2
  589.6 143.5 %all-reduce.14.cloned.1.call-start = ((), (), s32[]{:S(2)}) async-start(), calls=%async_computation.3 | async-start | bytes 2097152 | tf_op jit(solution)/shard_map/psum | solution.py:25
  688.8 97.6 %all-reduce.16.cloned.1.call-start = ((), (), s32[]{:S(2)}) async-start(), calls=%async_computation.4 | async-start | bytes 2097152 | tf_op jit(solution)/shard_map/psum | solution.py:25
  733.1 94.5 %all-gather.16.cloned.1.call-start = ((), (), s32[]{:S(2)}) async-start(), calls=%async_computation.11 | async-start | bytes 2621440 | tf_op jit(solution)/shard_map/all_gather | solution.py:19
  792.8 3.4 copy-start.3
  797.1 143.6 %all-reduce.18.cloned.1.call-start = ((), (), s32[]{:S(2)}) async-start(), calls=%async_computation.5 | async-start | bytes 2097152 | tf_op jit(solution)/shard_map/psum | solution.py:25
  896.2 97.5 %all-reduce.20.cloned.1.call-start = ((), (), s32[]{:S(2)}) async-start(), calls=%async_computation.6 | async-start | bytes 2097152 | tf_op jit(solution)/shard_map/psum | solution.py:25
  940.7 94.4 %all-gather.18.cloned.1.call-start = ((), (), s32[]{:S(2)}) async-start(), calls=%async_computation.12 | async-start | bytes 2621440 | tf_op jit(solution)/shard_map/all_gather | solution.py:19
  1000.2 3.4 copy-start.4
  1004.5 143.6 %all-reduce.22.cloned.1.call-start = ((), (), s32[]{:S(2)}) async-start(), calls=%async_computation.7 | async-start | bytes 2097152 | tf_op jit(solution)/shard_map/psum | solution.py:25
  1103.7 97.6 %all-reduce.24.cloned.1.call-start = ((), (), s32[]{:S(2)}) async-start(), calls=%async_computation.8 | async-start | bytes 2097152 | tf_op jit(solution)/shard_map/psum | solution.py:25
  1209.9 1.6 copy-start.1
  (1 other events, 0.8 us)
Sparse Core Ops, SparseCore 0:
  17.4 158.3 all-gather.9
  383.1 29.4 all-gather.11
  481.5 44.2 all-reduce.9
  528.1 50.7 all-reduce.11
  589.7 30.4 all-gather.13
  688.9 44.1 all-reduce.13
  735.6 50.7 all-reduce.15
  797.2 30.4 all-gather.15
  896.3 44.2 all-reduce.17
  943.0 50.7 all-reduce.19
  1004.6 30.4 all-gather.17
  1103.8 44.2 all-reduce.21
  1150.5 50.7 all-reduce.23
where the time goes:
time: 1230 us; the launch traced here: 1220 us
  waiting for transfers between devices  672 us (55%)
  other arithmetic  319 us (26%)
  local copies, waits for them, and re-layouts  144 us (12%)
  matrix products  58.6 us (5%)
  between operations  19.6 us (2%)
    psum x8, waiting for transfers between devices, broadcast_by_axis(): value = lax.psum(value, axis)  388 us
    all_gather x1, waiting for transfers between devices, local(): lax.all_gather(moved, ROW_COL, axis=1, tiled=True)  157 us
    another operation x28, other arithmetic, invert(): factor = jnp.linalg.cholesky(gram)  138 us
    all_gather x4, waiting for transfers between devices, from_root(): lax.all_gather(value, axis)  120 us
    unnamed x30, local copies, waits for them, and re-layouts  111 us
    scatter-add x1, other arithmetic, place_rows(): rows_d.at[local_row]  81 us
    another operation x9, other arithmetic, invert(): return jax.scipy.linalg.cho_solve((factor, True), block.T)  78.8 us
  transfers between devices with their start and end apart: 14, of which 14 were waited for; matrix products, arithmetic and copies ran while one was open for 0% of the time, Pallas kernels for 0%

commit v1 on v0

--- a/solution.py
+++ b/solution.py
@@ -8,6 +8,11 @@
 PANELS = 4
 COL = ("col_0", "col_1")
 ROW_COL = ("row", "col_0", "col_1")
+
+
+def gather_over(x, axis, d):
+    sent = jnp.stack([x] * lax.axis_size(axis))
+    return jnp.concatenate(lax.all_to_all(sent, axis, 0, 0), axis=d)
 
 
 def shifted(value, axis, by):
@@ -113,9 +118,7 @@
     place_rows, empty_carry = make_collector(
         blocks, row_offset, col_offset, row_width, col_width, rank_width, leaf_width
     )
-    collected = place_rows(
-        empty_carry, lax.all_gather(moved, ROW_COL, axis=1, tiled=True), jnp.int32(0)
-    )
+    collected = place_rows(empty_carry, gather_over(moved, ROW_COL, 1), jnp.int32(0))
     front = front_entries[0] + expand_tile(collected, counts, row_offset, col_offset, leaf_width)
     row_ids = row_offset + jnp.arange(row_width, dtype=jnp.int32)
     col_ids = col_offset + jnp.arange(col_width, dtype=jnp.int32)

time: 1230 us -> 1370 us (1.11)
  waiting for transfers between devices: 672 us -> 788 us
  local copies, waits for them, and re-layouts: 144 us -> 163 us
    all_to_all x0 -> x1, waiting for transfers between devices: none -> 251 us  [gather_over(): return jnp.concatenate(lax.all_to_all(sent, axis, 0, 0), axis=d)]
    all_gather x1 -> x0, waiting for transfers between devices: 157 us -> none  [local(): lax.all_gather(moved, ROW_COL, axis=1, tiled=True)]
    all_gather x4, waiting for transfers between devices: 120 us -> 142 us  [from_root(): lax.all_gather(value, axis)]
    all_to_all x0 -> x1, local copies, waits for them, and re-layouts: none -> 13.9 us  [gather_over(): return jnp.concatenate(lax.all_to_all(sent, axis, 0, 0), axis=d)]
    unnamed x30 -> x28, local copies, waits for them, and re-layouts: 111 us -> 110 us
where the time goes in v1:
time: 1370 us; the launch traced here: 1360 us
  waiting for transfers between devices  788 us (58%)
  other arithmetic  319 us (23%)
  local copies, waits for them, and re-layouts  163 us (12%)
  matrix products  58.6 us (4%)
  between operations  19.9 us (1%)
  starting transfers between devices  14.4 us (1%)
    psum x8, waiting for transfers between devices, broadcast_by_axis(): value = lax.psum(value, axis)  388 us
    all_to_all x1, waiting for transfers between devices, gather_over(): return jnp.concatenate(lax.all_to_all(sent, axis, 0, 0), axis=d)  251 us
    all_gather x4, waiting for transfers between devices, from_root(): lax.all_gather(value, axis)  142 us
    another operation x28, other arithmetic, invert(): factor = jnp.linalg.cholesky(gram)  138 us
    unnamed x28, local copies, waits for them, and re-layouts  110 us
    scatter-add x1, other arithmetic, place_rows(): rows_d.at[local_row]  81 us
    another operation x9, other arithmetic, invert(): return jax.scipy.linalg.cho_solve((factor, True), block.T)  78.8 us
  transfers between devices with their start and end apart: 14, of which 14 were waited for; matrix products, arithmetic and copies ran while one was open for 0% of the time, Pallas kernels for 0%

profile of v1, /device:TPU:1, one launch (start us, length us, event | category | flops | bytes accessed | tf_op | source)
XLA Modules:
  0.0 1364.2 jit_solution(3054898354999483302)
XLA Ops:
  34.1 251.5 %all-to-all-done = bf16[32,4,128,512]{3,2,1,0:T(8,128)(2,1)} async-done(((bf16[32,4,128,512]{3,2,1,0:T(8,128)(2,1)}), bf16[32,4,128,512]{3,2,1,0:T(8,128)(2,1)}, u32[]{:S(2)}, u32[]{:S(2)}) %all-to-all-start) | async-done | bytes 16777248 | tf_op jit(solution)/shard_map/all_to_all | solution.py:15
  285.6 13.9 %copy.38 = bf16[32,4,128,512]{3,2,0,1:T(8,128)(2,1)} copy(bf16[32,4,128,512]{3,2,1,0:T(8,128)(2,1)} %all-to-all-done) | data formatting | bytes 33554432 | tf_op jit(solution)/shard_map/all_to_all | solution.py:15
  312.6 81.0 %scatter_custom_fusion = f32[2048,256]{1,0:T(8,128)S(1)} fusion(s32[16384]{0:T(1024)S(1)} %bitcast.211, bf16[16384,256]{1,0:T(8,128)(2,1)} %bitcast.202, f32[]{:T(128)} %constant.285.clone.1), kind=kCustom, calls=%fused_computation.11 | custom fusion | flops 8388608 | bytes 10485764 | tf_op jit(solution)/shard_map/scatter-add | solution.py:65
  407.3 43.1 %scatter_custom_fusion.1 = bf16[8192,128]{1,0:T(8,128)(2,1)} fusion(s32[16384]{0:T(1024)S(1)} %bitcast.213, bf16[16384,128]{1,0:T(8,128)(2,1)} %bitcast.209, bf16[]{:T(256)} %constant.269.clone.1), kind=kCustom, calls=%fused_computation.55 | custom fusion | bytes 2097664
  452.2 41.6 %scatter_custom_fusion.2 = bf16[4096,128]{1,0:T(8,128)(2,1)S(1)} fusion(s32[16384]{0:T(1024)S(1)} %bitcast.212, bf16[16384,128]{1,0:T(8,128)(2,1)} %bitcast.208, bf16[]{:T(256)} %constant.269.clone.1), kind=kCustom, calls=%fused_computation.77 | custom fusion | bytes 1049088
  506.7 51.4 %all-gather.9.cloned.1.call-done = bf16[1024,1024]{1,0:T(8,128)(2,1)} async-done(((bf16[256,1024]{1,0:T(8,128)(2,1)}), bf16[1024,1024]{1,0:T(8,128)(2,1)}) %all-gather.9.cloned.1.call-update) | async-done | bytes 2097168 | tf_op jit(solution)/shard_map/all_gather | solution.py:24
  582.2 11.7 cholesky.231
  600.9 19.7 %custom-call.20 = f32[2,128,128]{1,2,0:T(8,128)S(1)} custom-call(f32[2,128,128]{2,1,0:T(8,128)S(1)} %get-tuple-element.81), custom_call_target="InvertDiagBlocksLowerTriangular" | custom-call | tf_op jit(solution)/shard_map/jit(_cho_solve)/triangular_solve | solution.py:37
  627.0 44.3 %all-reduce.10.cloned.1.call-done = bf16[2048,256]{1,0:T(8,128)(2,1)} async-done(((bf16[2048,256]{1,0:T(8,128)(2,1)}), bf16[2048,256]{1,0:T(8,128)(2,1)}) %all-reduce.10.cloned.1.call-update) | async-done | bytes 1048592 | tf_op jit(solution)/shard_map/psum | solution.py:30
  672.0 52.5 %all-reduce.12.cloned.1.call-done = bf16[2048,256]{1,0:T(8,128)(2,1)} async-done(((bf16[2048,256]{1,0:T(8,128)(2,1)}), bf16[2048,256]{1,0:T(8,128)(2,1)}) %all-reduce.12.cloned.1.call-update) | async-done | bytes 1048592 | tf_op jit(solution)/shard_map/psum | solution.py:30
  735.5 30.4 %all-gather.11.cloned.1.call-done = bf16[1024,1024]{1,0:T(8,128)(2,1)} async-done(((bf16[256,1024]{1,0:T(8,128)(2,1)}), bf16[1024,1024]{1,0:T(8,128)(2,1)}) %all-gather.11.cloned.1.call-update) | async-done | bytes 2097168 | tf_op jit(solution)/shard_map/all_gather | solution.py:24
  808.3 19.7 %custom-call.22 = f32[2,128,128]{1,2,0:T(8,128)S(1)} custom-call(f32[2,128,128]{2,1,0:T(8,128)S(1)} %get-tuple-element.82), custom_call_target="InvertDiagBlocksLowerTriangular" | custom-call | tf_op jit(solution)/shard_map/jit(_cho_solve)/triangular_solve | solution.py:37
  834.5 44.3 %all-reduce.14.cloned.1.call-done = bf16[2048,256]{1,0:T(8,128)(2,1)} async-done(((bf16[2048,256]{1,0:T(8,128)(2,1)}), bf16[2048,256]{1,0:T(8,128)(2,1)}) %all-reduce.14.cloned.1.call-update) | async-done | bytes 1048592 | tf_op jit(solution)/shard_map/psum | solution.py:30
  879.5 52.4 %all-reduce.16.cloned.1.call-done = bf16[2048,256]{1,0:T(8,128)(2,1)} async-done(((bf16[2048,256]{1,0:T(8,128)(2,1)}), bf16[2048,256]{1,0:T(8,128)(2,1)}) %all-reduce.16.cloned.1.call-update) | async-done | bytes 1048592 | tf_op jit(solution)/shard_map/psum | solution.py:30
  943.0 30.1 %all-gather.13.cloned.1.call-done = bf16[1024,1024]{1,0:T(8,128)(2,1)} async-done(((bf16[256,1024]{1,0:T(8,128)(2,1)}), bf16[1024,1024]{1,0:T(8,128)(2,1)}) %all-gather.13.cloned.1.call-update) | async-done | bytes 2097168 | tf_op jit(solution)/shard_map/all_gather | solution.py:24
  997.2 11.7 cholesky.299
  1015.6 19.7 %custom-call.24 = f32[2,128,128]{1,2,0:T(8,128)S(1)} custom-call(f32[2,128,128]{2,1,0:T(8,128)S(1)} %get-tuple-element.83), custom_call_target="InvertDiagBlocksLowerTriangular" | custom-call | tf_op jit(solution)/shard_map/jit(_cho_solve)/triangular_solve | solution.py:37
  1041.7 44.4 %all-reduce.18.cloned.1.call-done = bf16[2048,256]{1,0:T(8,128)(2,1)} async-done(((bf16[2048,256]{1,0:T(8,128)(2,1)}), bf16[2048,256]{1,0:T(8,128)(2,1)}) %all-reduce.18.cloned.1.call-update) | async-done | bytes 1048592 | tf_op jit(solution)/shard_map/psum | solution.py:30
  1086.9 52.5 %all-reduce.20.cloned.1.call-done = bf16[2048,256]{1,0:T(8,128)(2,1)} async-done(((bf16[2048,256]{1,0:T(8,128)(2,1)}), bf16[2048,256]{1,0:T(8,128)(2,1)}) %all-reduce.20.cloned.1.call-update) | async-done | bytes 1048592 | tf_op jit(solution)/shard_map/psum | solution.py:30
  1150.4 30.3 %all-gather.15.cloned.1.call-done = bf16[1024,1024]{1,0:T(8,128)(2,1)} async-done(((bf16[256,1024]{1,0:T(8,128)(2,1)}), bf16[1024,1024]{1,0:T(8,128)(2,1)}) %all-gather.15.cloned.1.call-update) | async-done | bytes 2097168 | tf_op jit(solution)/shard_map/all_gather | solution.py:24
  1204.8 11.7 cholesky.333
  1223.3 19.7 %custom-call.26 = f32[2,128,128]{1,2,0:T(8,128)S(1)} custom-call(f32[2,128,128]{2,1,0:T(8,128)S(1)} %get-tuple-element.84), custom_call_target="InvertDiagBlocksLowerTriangular" | custom-call | tf_op jit(solution)/shard_map/jit(_cho_solve)/triangular_solve | solution.py:37
  1249.4 44.4 %all-reduce.22.cloned.1.call-done = bf16[2048,256]{1,0:T(8,128)(2,1)} async-done(((bf16[2048,256]{1,0:T(8,128)(2,1)}), bf16[2048,256]{1,0:T(8,128)(2,1)}) %all-reduce.22.cloned.1.call-update) | async-done | bytes 1048592 | tf_op jit(solution)/shard_map/psum | solution.py:30
  1293.8 53.0 %all-reduce.24.cloned.1.call-done = bf16[2048,256]{1,0:T(8,128)(2,1)} async-done(((bf16[2048,256]{1,0:T(8,128)(2,1)}), bf16[2048,256]{1,0:T(8,128)(2,1)}) %all-reduce.24.cloned.1.call-update) | async-done | bytes 1048592 | tf_op jit(solution)/shard_map/psum | solution.py:30
  (229 shorter events, 284.5 us)
Async XLA Ops:
  6.5 26.4 %copy-start = (s32[16,16]{1,0:T(8,128)S(1)}, s32[16,16]{1,0:T(8,128)}, u32[]{:S(2)}) copy-start(s32[16,16]{1,0:T(8,128)} %param.22) | copy-start | bytes 3076
  7.6 8.8 collective-permute-start
  22.4 11.1 copy-start.8
  22.4 11.2 copy-start.6
  22.4 11.2 copy-start.7
  22.4 263.2 %all-to-all-start = ((bf16[32,4,128,512]{3,2,1,0:T(8,128)(2,1)}), bf16[32,4,128,512]{3,2,1,0:T(8,128)(2,1)}, u32[]{:S(2)}, u32[]{:S(2)}) async-start(bf16[32,4,128,512]{3,2,1,0:T(8,128)(2,1)} %stack.2), calls=%async_computation | async-start | bytes 33554432 | tf_op jit(solution)/shard_map/all_to_all | solution.py:15
  32.9 1.0 copy-start.9
  32.9 525.2 %all-gather.9.cloned.1.call-start = ((), (), s32[]{:S(2)}) async-start(), calls=%async_computation.9 | async-start | bytes 2621440 | tf_op jit(solution)/shard_map/all_gather | solution.py:24
  502.3 3.4 copy-start.5
  506.6 164.7 %all-reduce.10.cloned.1.call-start = ((), (), s32[]{:S(2)}) async-start(), calls=%async_computation.1 | async-start | bytes 2097152 | tf_op jit(solution)/shard_map/psum | solution.py:30
  626.9 97.6 %all-reduce.12.cloned.1.call-start = ((), (), s32[]{:S(2)}) async-start(), calls=%async_computation.2 | async-start | bytes 2097152 | tf_op jit(solution)/shard_map/psum | solution.py:30
  671.3 94.5 %all-gather.11.cloned.1.call-start = ((), (), s32[]{:S(2)}) async-start(), calls=%async_computation.10 | async-start | bytes 2621440 | tf_op jit(solution)/shard_map/all_gather | solution.py:24
  730.9 3.4 copy-start.2
  735.2 143.5 %all-reduce.14.cloned.1.call-start = ((), (), s32[]{:S(2)}) async-start(), calls=%async_computation.3 | async-start | bytes 2097152 | tf_op jit(solution)/shard_map/psum | solution.py:30
  834.4 97.4 %all-reduce.16.cloned.1.call-start = ((), (), s32[]{:S(2)}) async-start(), calls=%async_computation.4 | async-start | bytes 2097152 | tf_op jit(solution)/shard_map/psum | solution.py:30
  878.8 94.4 %all-gather.13.cloned.1.call-start = ((), (), s32[]{:S(2)}) async-start(), calls=%async_computation.11 | async-start | bytes 2621440 | tf_op jit(solution)/shard_map/all_gather | solution.py:24
  938.3 3.4 copy-start.3
  942.6 143.6 %all-reduce.18.cloned.1.call-start = ((), (), s32[]{:S(2)}) async-start(), calls=%async_computation.5 | async-start | bytes 2097152 | tf_op jit(solution)/shard_map/psum | solution.py:30
  1041.7 97.7 %all-reduce.20.cloned.1.call-start = ((), (), s32[]{:S(2)}) async-start(), calls=%async_computation.6 | async-start | bytes 2097152 | tf_op jit(solution)/shard_map/psum | solution.py:30
  1086.2 94.5 %all-gather.15.cloned.1.call-start = ((), (), s32[]{:S(2)}) async-start(), calls=%async_computation.12 | async-start | bytes 2621440 | tf_op jit(solution)/shard_map/all_gather | solution.py:24
  1145.8 3.4 copy-start.4
  1150.1 143.6 %all-reduce.22.cloned.1.call-start = ((), (), s32[]{:S(2)}) async-start(), calls=%async_computation.7 | async-start | bytes 2097152 | tf_op jit(solution)/shard_map/psum | solution.py:30
  1249.3 97.5 %all-reduce.24.cloned.1.call-start = ((), (), s32[]{:S(2)}) async-start(), calls=%async_computation.8 | async-start | bytes 2097152 | tf_op jit(solution)/shard_map/psum | solution.py:30
  1355.4 1.6 copy-start.1
Sparse Core Ops, SparseCore 0:
  506.7 51.3 all-gather.8
  627.0 44.2 all-reduce.9
  673.8 50.7 all-reduce.11
  735.4 30.4 all-gather.10
  834.5 44.1 all-reduce.13
  881.1 50.7 all-reduce.15
  942.7 30.4 all-gather.12
  1041.8 44.3 all-reduce.17
  1088.6 50.7 all-reduce.19
  1150.3 30.4 all-gather.14
  1249.5 44.2 all-reduce.21
  1296.1 50.7 all-reduce.23
